TPU v7x, 256 devices: a whole 4x4x8 slice. The times are simulated.
256 devices in a mesh: rows: 64 (over z, x, core), cols: 4 (over y).
Axes of the slice: x: 4, y: 4, z: 8, core: 2. Of those that a mesh axis runs over, the one named last changes fastest.
Arguments:
- source: float32 [8192, 32768], P('rows', 'cols'), may hold values from -6 to 6
- low_row: int32 [8192], replicated, may hold values from 0 to 8190, as said below
- weight_low: float32 [8192], replicated, may hold values from 0 to 1
Outputs:
- mercator: float32 [8192, 32768], P('rows', 'cols')
- level1: float32 [4096, 16384], P('rows', 'cols')
- level2: float32 [2048, 8192], P('rows', 'cols')
- level3: float32 [1024, 4096], P(('rows', 'cols'))
- level4: float32 [512, 2048], P(('rows', 'cols'))
Inputs may be any that keep to these rules, and one draw needn't show every extreme that they name: With t = 68 degrees in radians, E = ln tan(pi/4 + t/2), y = E * (1 - (2m + 1) / 16384) and lat = 2 atan(exp(y)) - pi/2, the base row of Mercator row m is floor((t - lat) / t * 8192 - 0.5) clipped to the range; low_row[m] differs from it by at most 2 and is then clipped to the range.
All inputs are finite; a program needn't handle non-finite values.
Results may differ from a plain program's by a relative error of at most 0.00007.
Values sent between devices are 32-bit elements; how exact they have to be, the bound alone decides.
No kernel may reach another device: no remote copies, remote signals or barrier semaphores. Data moves between devices by JAX's collectives and lax.ppermute only.
A program may use at most 128 MiB of HBM per device.

v0:
```python
import math

import jax
import jax.numpy as jnp
import numpy as np
from jax import lax
from jax.experimental import pallas as pl
from jax.experimental.pallas import tpu as pltpu
from jax.sharding import PartitionSpec as P


TOTAL = 8192
ROWS = 64
OWN = TOTAL // ROWS
SLOTS = (9, 10, 11, 12, 0, 1, 2, 3, 4, 5, 6, 7, 8)
ISSUE = (0, 2, 4, 6, 8, 10, 12, 14, 16, 18, 20, 22, 24, 1, 3, 5, 7)
SPAN = 3
CODE = 1024

STOPS = {
    "D": (),
    "P": ((0, 1),),
    "M": ((0, -1),),
    "V": ((1, -1),),
    "Y": ((-1, -1),),
}
CLASSES = (("D", 32, 3), ("D", 16, 3), ("D", 8, 3), ("P", 32, 1), ("M", 32, 1), ("Y", 16, 1), ("V", 16, 1))
ROUTES = (
    2, 65, 513, 545, 578, 33313, 33794, 33825, 34305, 34337, 34369, 67105,
    67137, 67586, 67617, 68097, 68161, 100865, 100930, 101378, 101409, 101441, 101921, 134657,
    134690, 134722, 135170, 167937, 168449, 168482, 168515, 168961, 201762, 201793, 201825, 202242,
    202305, 235073, 235169, 235522, 235554, 236065, 236097, 268802, 268833, 269313, 269345, 269378,
    302114, 302145, 302595, 303169, 335425, 335874, 335937, 336001, 336385, 336449, 369186, 369217,
    369281, 369666, 402467, 402947, 435779, 436226, 436353, 436385, 436769, 469507, 469569, 470049,
    470082, 502786, 502817, 502849, 503329, 503361, 503393, 536065, 536098, 536129, 536578, 536641,
    569345, 569377, 569409, 569858, 569889, 569921, 602658, 602689, 603139, 635937, 635970, 636418,
    636450, 636481, 669217, 669249, 669698, 669730, 669762, 702497, 702979, 703043, 735777, 736258,
    736290, 736353, 769090, 769539, 769570, 802370, 802819, 802849, 802881, 835617, 836098, 836130,
    836162, 868897, 868929, 869378, 869410, 869442, 902145, 902657, 902691, 902722, 935425, 935489,
    935938, 935969, 936001, 968705, 968737, 969217, 969250, 969282, 1001986, 1002497, 1002529, 1002562,
    1035266, 1035297, 1035777, 1035842, 1068546, 1068578, 1069057, 1101826, 1101859, 1102402, 1135107, 1135137,
    1135169, 1167905, 1168386, 1168418, 1168449, 1201153, 1201217, 1201665, 1201699, 1234434, 1234945, 1234977,
    1235009, 1267714, 1267745, 1267777, 1268258, 1300995, 1301025, 1301569, 1333825, 1334275, 1334338, 1367074,
    1367554, 1367713, 1400353, 1400385, 1400417, 1400897, 1400961, 1400993, 1433601, 1433635, 1433665, 1434177,
    1434273, 1466883, 1466913, 1499681, 1500163, 1532962, 1532993, 1533442, 1566209, 1566273, 1566305, 1566721,
    1566785, 1599490, 1599521, 1599553, 1599681, 1632321, 1632771, 1632833, 1665570, 1665601, 1666049, 1666113,
    1666209, 1666241, 1698818, 1698881, 1699361, 1699393, 1699521, 1732098, 1732130, 1732161, 1764929, 1765378,
    1765409, 1765537, 1798178, 1798209, 1798657, 1798753, 1831426, 1831457, 1831969, 1832002, 1864707, 1864769,
    1897505, 1897986, 1898017, 1898049, 1930753, 1930785, 1930817, 1931265, 1931297, 1931329, 1964034, 1964065,
    1964097, 1964610, 1997314, 1997346, 1997377, 2030081, 2030593, 2030626, 2030658, 2063362, 2063873, 2063937,
    2096642, 2096674,
)


def row_bounds():
    top = 68.0 * math.pi / 180.0
    edge = math.log(math.tan(math.pi / 4 + top / 2))
    y = edge * (1 - (2 * np.arange(TOTAL) + 1) / (2.0 * TOTAL))
    position = (top - (2 * np.arctan(np.exp(y)) - math.pi / 2)) / top * TOTAL - 0.5
    low = np.clip(np.floor(position - 0.05), 0, TOTAL - 2) - 2
    high = np.clip(np.floor(position + 0.05), 0, TOTAL - 2) + 2
    return np.clip(low, 0, TOTAL - 2).astype(int), np.clip(high, 0, TOTAL - 2).astype(int)


def wanted(low, high):
    out = {}
    for d in range(ROWS):
        mine = range(OWN * d, OWN * d + OWN)
        first, last = low[mine[0]], high[mine[-1]] + 1
        for s in range(first // OWN, last // OWN + 1):
            begin, end = s * OWN, s * OWN + OWN - 1
            plain = [("s", r) for r in range(max(first, begin), min(last, end) + 1)]
            inside = [m for m in mine if low[m] >= begin and high[m] + 1 <= end]
            across = sorted({
                r for m in mine if m not in inside for r in range(low[m], high[m] + 2) if r // OWN == s
            })
            mixed = [("s", r) for r in across if r < begin + OWN // 2]
            mixed += [("m", m) for m in inside]
            mixed += [("s", r) for r in across if r >= begin + OWN // 2]
            out[s, d] = plain if len(plain) <= len(mixed) else mixed
    return out


def stop(q, dz, dx):
    z, x = q // 8, q % 8 // 2
    return (z + dz) % 8 * 8 + (x + dx) % 4 * 2 + q % 2


def colour(edges, count):
    at_s, at_d = {}, {}
    for s, d in edges:
        a = next(c for c in range(count) if (s, c) not in at_s)
        b = next(c for c in range(count) if (d, c) not in at_d)
        if a != b:
            path, node, side, c = [], d, 1, a
            while True:
                table = at_d if side else at_s
                if (node, c) not in table:
                    break
                other = table[node, c]
                path.append((other, node, c) if side else (node, other, c))
                node, side, c = other, 1 - side, a + b - c
            for u, v, k in path:
                del at_s[u, k], at_d[v, k]
            for u, v, k in path:
                at_s[u, a + b - k], at_d[v, a + b - k] = v, u
        at_s[s, a], at_d[d, a] = d, s
    return [sorted((s, d) for (s, k), d in at_s.items() if k == c) for c in range(count)]


def make_plan():
    low, high = row_bounds()
    items = wanted(low, high)
    by_class = [[] for _ in CLASSES]
    for code in ROUTES:
        blocks, kind, d, s = code % 32, code // 32 % 16, code // 512 % 64, code // 32768
        by_class[kind] += [(s, d)] * blocks
    slots, left = [], {e: list(v) for e, v in items.items()}
    for (kind, size, count), edges in zip(CLASSES, by_class):
        for pairs in colour(edges, count):
            slots.append((kind, size, pairs))
    slots = [slots[j] for j in SLOTS]
    total = sum(size for _, size, _ in slots)
    send = np.zeros((ROWS, 1, total), np.int32)
    sends = np.zeros((ROWS, len(slots)), np.int32)
    near = np.full(ROWS, ROWS - SPAN)
    merc = np.full((ROWS, OWN), -1, np.int32)
    base = np.array([low[OWN * d] for d in range(ROWS)])
    width = max(high[OWN * d + OWN - 1] + 2 - base[d] for d in range(ROWS))
    place = np.zeros((ROWS, width), np.int32)
    used = np.zeros((ROWS, len(slots)), np.int32)
    at = 0
    for j, (kind, size, pairs) in enumerate(slots):
        for s, d in pairs:
            block, left[s, d] = left[s, d][:size], left[s, d][size:]
            used[d, j] = sends[s, j] = 1 if block else 0
            for k, (what, r) in enumerate(block):
                if what == "m":
                    send[s, 0, at + k] = CODE + r
                    near[s] = min(near[s], d)
                    merc[d, r - OWN * d] = at + k
                else:
                    send[s, 0, at + k] = r - OWN * s
                    place[d, r - base[d]] = at + k
        at += size
    assert not any(left.values())
    take = np.concatenate([used, base[:, None].astype(np.int32), merc, place], axis=1)[:, None, :]
    for s in range(ROWS):
        codes = send[s, 0]
        codes[codes >= CODE] -= OWN * near[s]
        assert codes.max() < CODE + SPAN * OWN
    send = np.concatenate([near[:, None, None], sends[:, None, :], send], axis=2)
    return slots, send.astype(np.int32), take.astype(np.int32)


def hops(slot):
    kind, _, pairs = slot
    tracks = []
    for s, d in pairs:
        track = [s]
        for dz, dx in STOPS[kind]:
            track.append(stop(track[-1], dz, dx))
        tracks.append(track + [d])
    return [[(t[i], t[i + 1]) for t in tracks] for i in range(len(tracks[0]) - 1)]


def pack_rows(slots, group, source, send, me, low_row, weight_low):
    starts = np.cumsum([1 + len(slots)] + [size for _, size, _ in slots])
    sizes = [slots[j][1] for j in group]

    def kernel(me_ref, send_ref, low_ref, weight_ref, source_ref, *refs):
        outs, (lows, weights, sems) = refs[: len(group)], refs[len(group) :]
        begin = me_ref[0] * OWN
        near = send_ref[0, 0, 0]
        copies = [
            pltpu.make_async_copy(low_ref.at[pl.ds(near, SPAN)], lows, sems.at[0]),
            pltpu.make_async_copy(weight_ref.at[pl.ds(near, SPAN)], weights, sems.at[1]),
        ]
        for copy in copies:
            copy.start()
        for copy in copies:
            copy.wait()
        for j, out, size in zip(group, outs, sizes):

            def row(k, _, out=out, at=int(starts[j])):
                code = send_ref[0, 0, at + k]
                mixed = code >= CODE
                m = jnp.maximum(code - CODE, 0)
                a, b = lax.shift_right_logical(m, 7), lax.bitwise_and(m, OWN - 1)
                r0 = jnp.where(mixed, jnp.clip(lows[a, 0, b] - begin, 0, OWN - 2), code)
                r1 = jnp.where(mixed, r0 + 1, r0)
                w = jnp.where(mixed, weights[a, 0, b], 1.0)
                v = 1.0 - w
                b0 = lax.shift_right_logical(r0, 3) * 512 + lax.bitwise_and(r0, 7)
                b1 = lax.shift_right_logical(r1, 3) * 512 + lax.bitwise_and(r1, 7)
                for c in range(8):
                    x = source_ref[pl.ds(b0 + 64 * c, 8, stride=8), :]
                    y = source_ref[pl.ds(b1 + 64 * c, 8, stride=8), :]
                    out[pl.ds(pl.multiple_of(k * 64 + 8 * c, 8), 8), :] = w * x + v * y
                return 0

            @pl.when(send_ref[0, 0, 1 + j] > 0)
            def _(row=row, size=size):
                lax.fori_loop(0, size, row, 0, unroll=8)

    total = send.shape[-1]
    return pl.pallas_call(
        kernel,
        grid_spec=pltpu.PrefetchScalarGridSpec(
            num_scalar_prefetch=1,
            grid=(1,),
            in_specs=[
                pl.BlockSpec((1, 1, total), lambda i, q: (q[0], 0, 0), memory_space=pltpu.SMEM),
                pl.BlockSpec(memory_space=pl.ANY),
                pl.BlockSpec(memory_space=pl.ANY),
                pl.BlockSpec(memory_space=pltpu.VMEM),
            ],
            out_specs=[pl.BlockSpec(memory_space=pltpu.VMEM) for _ in sizes],
            scratch_shapes=[
                pltpu.SMEM((SPAN, 1, OWN), jnp.int32),
                pltpu.SMEM((SPAN, 1, OWN), jnp.float32),
                pltpu.SemaphoreType.DMA((2,)),
            ],
        ),
        out_shape=[pltpu.VMEM((size * 64, 128), jnp.float32) for size in sizes],
        compiler_params=pltpu.CompilerParams(vmem_limit_bytes=8 << 20),
        name="pack_rows",
    )(me, send, low_row, weight_low, source)


def finish(slots, blocks, take, me, low_row, weight_low):
    sizes = [size for _, size, _ in slots]
    starts = np.cumsum([0] + sizes)
    n = len(slots)
    width = take.shape[-1] - n - 1 - OWN

    def pooled(sums, first, rows):
        pair = jnp.concatenate(
            [sums[pl.ds(first, rows // 2, stride=2), :], sums[pl.ds(first + 1, rows // 2, stride=2), :]], axis=1
        )
        lane = lax.broadcasted_iota(jnp.int32, (256, 128), 0)
        to = lax.broadcasted_iota(jnp.int32, (256, 128), 1)
        pairing = jnp.where(lax.div(lane, 2) == to, 0.25, 0.0).astype(jnp.bfloat16)
        high = pair.astype(jnp.bfloat16)
        low = (pair - high.astype(jnp.float32)).astype(jnp.bfloat16)
        return sum(jnp.dot(part, pairing, preferred_element_type=jnp.float32) for part in (low, high))

    def kernel(me_ref, take_ref, low_ref, weight_ref, *refs):
        ins, (out, out1, out2, *smalls), (got, sums, ones, sems) = refs[:n], refs[n : n + 7], refs[n + 7 :]
        step = pl.program_id(0)

        @pl.when(step == 0)
        def _():
            def copy(j):
                return pltpu.make_async_copy(ins[j], got.at[pl.ds(int(starts[j]) * 64, sizes[j] * 64), :], sems.at[j])

            for j in range(n):

                @pl.when(take_ref[0, 0, j] > 0)
                def _(j=j):
                    copy(j).start()

            for j in range(n):

                @pl.when(take_ref[0, 0, j] > 0)
                def _(j=j):
                    copy(j).wait()

        base = take_ref[0, 0, n]

        def blended(r):
            i = step * 32 + r
            fixed = take_ref[0, 0, n + 1 + i]
            c = jnp.clip(low_ref[0, 0, i] - base, 0, width - 2)
            p0 = take_ref[0, 0, n + 1 + OWN + c]
            p1 = take_ref[0, 0, n + 2 + OWN + c]
            done = fixed >= 0
            p0 = jnp.where(done, fixed, p0)
            p1 = jnp.where(done, fixed, p1)
            w = jnp.where(done, 1.0, weight_ref[0, 0, i])
            v = 1.0 - w
            for j in range(8):
                a = got[pl.ds(pl.multiple_of(p0 * 64 + 8 * j, 8), 8), :]
                b = got[pl.ds(pl.multiple_of(p1 * 64 + 8 * j, 8), 8), :]
                yield j, w * a + v * b

        for r in range(0, 32, 2):
            for (j, a), (_, b) in zip(blended(r), blended(r + 1)):
                out[pl.ds(r // 8 * 512 + r % 8 + 64 * j, 8, stride=8), :] = a
                out[pl.ds(r // 8 * 512 + r % 8 + 1 + 64 * j, 8, stride=8), :] = b
                sums[pl.ds(r * 32 + 8 * j, 8), :] = a + b
        for half in range(2):
            one = pooled(sums, half * 512, 512)
            for r in range(8):
                for j in range(4):
                    out1[pl.ds(half * 256 + r + 64 * j, 8, stride=8), :] = one[r * 32 + 8 * j : r * 32 + 8 * j + 8]
            for r in range(4):
                ones[pl.ds(step * 256 + half * 128 + r * 32, 32), :] = (
                    one[r * 64 : r * 64 + 32] + one[r * 64 + 32 : r * 64 + 64]
                )

        @pl.when(step == 3)
        def _():
            two = pooled(ones, 0, 1024)
            for r in range(32):
                for j in range(2):
                    out2[pl.ds(r // 8 * 128 + r % 8 + 64 * j, 8, stride=8), :] = two[r * 16 + 8 * j : r * 16 + 8 * j + 8]
            for r in range(16):
                sums[pl.ds(r * 16, 16), :] = two[r * 32 : r * 32 + 16] + two[r * 32 + 16 : r * 32 + 32]
            three = pooled(sums, 0, 256)
            ones[pl.ds(0, 128), :] = three
            for r in range(8):
                sums[pl.ds(r * 8, 8), :] = three[r * 16 : r * 16 + 8] + three[r * 16 + 8 : r * 16 + 16]
            ones[pl.ds(128, 32), :] = pooled(sums, 0, 64)
            for k, small in enumerate(smalls):
                c = lax.rem(me_ref[1] + k, 4)
                small[pl.ds(0, 32), :] = ones[pl.ds(pl.multiple_of(c * 32, 8), 32), :]
                small[pl.ds(32, 8), :] = ones[pl.ds(pl.multiple_of(128 + c * 8, 8), 8), :]

    return pl.pallas_call(
        kernel,
        grid_spec=pltpu.PrefetchScalarGridSpec(
            num_scalar_prefetch=1,
            grid=(4,),
            in_specs=[
                pl.BlockSpec((1, 1, take.shape[-1]), lambda i, q: (q[0], 0, 0), memory_space=pltpu.SMEM),
                pl.BlockSpec((1, 1, OWN), lambda i, q: (q[0], 0, 0), memory_space=pltpu.SMEM),
                pl.BlockSpec((1, 1, OWN), lambda i, q: (q[0], 0, 0), memory_space=pltpu.SMEM),
            ]
            + [pl.BlockSpec(memory_space=pl.ANY)] * n,
            out_specs=[
                pl.BlockSpec((2048, 128), lambda i, q: (i, 0)),
                pl.BlockSpec((512, 128), lambda i, q: (i, 0)),
                pl.BlockSpec((512, 128), lambda i, q: (0, 0)),
            ]
            + [pl.BlockSpec((40, 128), lambda i, q: (0, 0))] * 4,
            scratch_shapes=[
                pltpu.VMEM((int(starts[-1]) * 64, 128), jnp.float32),
                pltpu.VMEM((1024, 128), jnp.float32),
                pltpu.VMEM((1024, 128), jnp.float32),
                pltpu.SemaphoreType.DMA((n,)),
            ],
        ),
        out_shape=[
            jax.ShapeDtypeStruct((8192, 128), jnp.float32),
            jax.ShapeDtypeStruct((2048, 128), jnp.float32),
            jax.ShapeDtypeStruct((512, 128), jnp.float32),
        ]
        + [jax.ShapeDtypeStruct((40, 128), jnp.float32)] * 4,
        compiler_params=pltpu.CompilerParams(dimension_semantics=("arbitrary",), vmem_limit_bytes=20 << 20),
        name="finish",
    )(me, take, low_row, weight_low, *blocks)


def join(pieces, me):
    def kernel(me_ref, *refs):
        ins, (three, four) = refs[:4], refs[4:]
        for k, piece in enumerate(ins):
            c = lax.rem(me_ref[1] + 4 - k, 4)
            for t in range(8):
                three[:, pl.ds(pl.multiple_of(c * 1024 + 128 * t, 128), 128)] = piece[pl.ds(t, 4, stride=8), :]
            for t in range(4):
                four[:, pl.ds(pl.multiple_of(c * 512 + 128 * t, 128), 128)] = piece[pl.ds(32 + t, 2, stride=4), :]

    return pl.pallas_call(
        kernel,
        in_specs=[pl.BlockSpec(memory_space=pltpu.SMEM)] + [pl.BlockSpec(memory_space=pltpu.VMEM)] * 4,
        out_shape=[jax.ShapeDtypeStruct((4, 4096), jnp.float32), jax.ShapeDtypeStruct((2, 2048), jnp.float32)],
        compiler_params=pltpu.CompilerParams(vmem_limit_bytes=4 << 20),
        name="join",
    )(me, *pieces)


def tiled(flat, rows, cols):
    return flat.reshape(rows // 8, cols // 128, 8, 128).transpose(0, 2, 1, 3).reshape(rows, cols)


def solution(mesh):
    slots, send, take = make_plan()
    groups = [range(3), range(3, len(slots))]
    order = [divmod(code, 2) for code in ISSUE]

    def body(source, low_row, weight_low):
        me = jnp.stack([lax.axis_index("rows"), lax.axis_index("cols")]).astype(jnp.int32)
        flat = source.reshape(16, 8, 64, 128).transpose(0, 2, 1, 3).reshape(TOTAL, 128)
        flat = pltpu.with_memory_space_constraint(flat, pltpu.VMEM)
        low_row = low_row.reshape(ROWS, 1, OWN)
        weight_low = weight_low.reshape(ROWS, 1, OWN)
        low_row = pltpu.with_memory_space_constraint(low_row, pltpu.HBM)
        weight_low = pltpu.with_memory_space_constraint(weight_low, pltpu.HBM)
        sends = pltpu.with_memory_space_constraint(jnp.asarray(send), pltpu.HBM)
        takes = pltpu.with_memory_space_constraint(jnp.asarray(take), pltpu.HBM)
        packed = []
        for group in groups:
            packed += pack_rows(slots, group, flat, sends, me, low_row, weight_low)
        blocks = [[b] for b in packed]
        tracks = [hops(slot) for slot in slots]
        for j, i in order:
            blocks[j].append(lax.ppermute(blocks[j][-1], "rows", tracks[j][i]))
        out, out1, out2, *smalls = finish(slots, [b[-1] for b in blocks], takes, me, low_row, weight_low)
        pieces = smalls[:1]
        for k in (2, 1, 3):
            pieces.append(lax.ppermute(smalls[k], "cols", [(c, (c + k) % 4) for c in range(4)]))
        level3, level4 = join([pieces[0], pieces[2], pieces[1], pieces[3]], me)
        return (
            tiled(out, 128, 8192),
            tiled(out1, 64, 4096),
            tiled(out2, 32, 2048),
            level3,
            level4,
        )

    return jax.shard_map(
        body,
        mesh=mesh,
        in_specs=(P("rows", "cols"), P(), P()),
        out_specs=(
            P("rows", "cols"),
            P("rows", "cols"),
            P("rows", "cols"),
            P(("rows", "cols"), None),
            P(("rows", "cols"), None),
        ),
        check_vma=False,
    )
```

profile of v0, /device:TPU:194, one launch (start us, length us, event | category | flops | bytes accessed | tf_op | source)
XLA Modules:
  0.0 150.9 jit_solution(17907526986417644814)
XLA Ops:
  0.7 2.2 %copy-done = f32[128,8192]{1,0:T(8,128)S(1)} copy-done((f32[128,8192]{1,0:T(8,128)S(1)}, f32[128,8192]{1,0:T(8,128)}, u32[]{:S(2)}) %copy-start) | copy-done | bytes 4194328
  2.9 2.3 %pack_rows.2 = (f32[2048,128]{1,0:T(8,128)S(1)}, f32[2048,128]{1,0:T(8,128)S(1)}, f32[1024,128]{1,0:T(8,128)S(1)}) custom-call(s32[2]{0:T(128)S(1)} %pad_add_fusion.me_ref, s32[64,1,278]{2,1,0:T(1,128)} %constant.13.clone.send_ref, s32[64,1,128]{2,1,0:T(1,128)} %bitcast.26, f32[64,1,128]{2,1,0:T(1,128)} %bitcast.29, f32[8192,128]{1,0:T(8,128)S(1)} %bitcast.24), custom_call_target="tpu_custom_call" | custom-call | tf_op jit(solution)/shard_map/pack_rows/pallas_call | solution.py:207
  5.2 2.6 %collective-permute-start.4 = (f32[1024,128]{1,0:T(8,128)S(1)}, f32[1024,128]{1,0:T(8,128)S(1)}, u32[]{:S(2)}, u32[]{:S(2)}) collective-permute-start(f32[1024,128]{1,0:T(8,128)S(1)} %get-tuple-element.29), channel_id=1, source_target_pairs={{28,244},{52,12},{164,156},{168,128},{172,132},{200,160},{212,172}... | collective-permute-start | bytes 1572872 | tf_op jit(solution)/shard_map/ppermute | solution.py:399
  7.8 3.9 %pack_rows.3 = (f32[1024,128]{1,0:T(8,128)S(1)}, f32[2048,128]{1,0:T(8,128)S(1)}, f32[2048,128]{1,0:T(8,128)S(1)}, f32[2048,128]{1,0:T(8,128)S(1)}, f32[1024,128...) custom-call(s32[2]{0:T(128)S(1)} %pad_add_fusion.me_ref, ...), custom_call_target="tpu_custom_call" | custom-call | tf_op jit(solution)/shard_map/pack_rows/pallas_call | solution.py:207
  11.7 2.7 %collective-permute-start.14 = (f32[512,128]{1,0:T(8,128)S(1)}, f32[512,128]{1,0:T(8,128)S(1)}, u32[]{:S(2)}, u32[]{:S(2)}) collective-permute-start(f32[512,128]{1,0:T(8,128)S(1)} %get-tuple-element.37), channel_id=1, source_target_pairs={{0,0},{8,12},{12,20},{16,28},{20,36},{24,40},{28,44},{32,56},{36,6... | collective-permute-start | bytes 786440 | tf_op jit(solution)/shard_map/ppermute | solution.py:399
  14.5 2.1 %collective-permute-start.15 = (f32[512,128]{1,0:T(8,128)S(1)}, f32[512,128]{1,0:T(8,128)S(1)}, u32[]{:S(2)}, u32[]{:S(2)}) collective-permute-start(f32[512,128]{1,0:T(8,128)S(1)} %get-tuple-element.38), channel_id=1, source_target_pairs={{0,4},{4,12},{12,20},{16,28},{20,36},{24,44},{28,52},{36,56},{40,6... | collective-permute-start | bytes 786440 | tf_op jit(solution)/shard_map/ppermute | solution.py:399
  17.3 1.3 collective-permute-start.6
  18.6 13.3 %collective-permute-done.14.refs_10_ = f32[512,128]{1,0:T(8,128)S(1)} collective-permute-done((f32[512,128]{1,0:T(8,128)S(1)}, f32[512,128]{1,0:T(8,128)S(1)}, u32[]{:S(2)}, u32[]{:S(2)}) %collective-permute-start.14) | collective-permute-done | bytes 262176 | tf_op jit(solution)/shard_map/ppermute | solution.py:399
  31.9 3.8 %collective-permute-start.11 = (f32[1024,128]{1,0:T(8,128)S(1)}, f32[1024,128]{1,0:T(8,128)S(1)}, u32[]{:S(2)}, u32[]{:S(2)}) collective-permute-start(f32[1024,128]{1,0:T(8,128)S(1)} %get-tuple-element.34), channel_id=1, source_target_pairs={{4,4},{8,12},{12,24},{16,28},{20,36},{24,40},{28,48},{32,52},{36,5... | collective-permute-start | bytes 1572872 | tf_op jit(solution)/shard_map/ppermute | solution.py:399
  35.7 9.1 %collective-permute-done.15.refs_11_ = f32[512,128]{1,0:T(8,128)S(1)} collective-permute-done((f32[512,128]{1,0:T(8,128)S(1)}, f32[512,128]{1,0:T(8,128)S(1)}, u32[]{:S(2)}, u32[]{:S(2)}) %collective-permute-start.15) | collective-permute-done | bytes 262176 | tf_op jit(solution)/shard_map/ppermute | solution.py:399
  46.3 1.9 %collective-permute-start.12 = (f32[1024,128]{1,0:T(8,128)S(1)}, f32[1024,128]{1,0:T(8,128)S(1)}, u32[]{:S(2)}, u32[]{:S(2)}) collective-permute-start(f32[1024,128]{1,0:T(8,128)S(1)} %get-tuple-element.35), channel_id=1, source_target_pairs={{0,4},{4,8},{8,16},{16,28},{20,36},{24,40},{28,48},{36,56},{44,68}... | collective-permute-start | bytes 1572872 | tf_op jit(solution)/shard_map/ppermute | solution.py:399
  49.7 10.1 %collective-permute-done.12.refs_8_ = f32[1024,128]{1,0:T(8,128)S(1)} collective-permute-done((f32[1024,128]{1,0:T(8,128)S(1)}, f32[1024,128]{1,0:T(8,128)S(1)}, u32[]{:S(2)}, u32[]{:S(2)}) %collective-permute-start.12) | collective-permute-done | bytes 524320 | tf_op jit(solution)/shard_map/ppermute | solution.py:399
  60.5 1.3 collective-permute-start.8
  61.8 1.3 collective-permute-start.9
  63.1 11.8 %collective-permute-start.10 = (f32[2048,128]{1,0:T(8,128)S(1)}, f32[2048,128]{1,0:T(8,128)S(1)}, u32[]{:S(2)}, u32[]{:S(2)}) collective-permute-start(f32[2048,128]{1,0:T(8,128)S(1)} %get-tuple-element.33), channel_id=1, source_target_pairs={{0,4},{4,12},{8,20},{12,24},{16,32},{20,40},{32,56},{36,60},{40,68... | collective-permute-start | bytes 3145736 | tf_op jit(solution)/shard_map/ppermute | solution.py:399
  76.4 13.2 %collective-permute-done.8.refs_4_ = f32[2048,128]{1,0:T(8,128)S(1)} collective-permute-done((f32[2048,128]{1,0:T(8,128)S(1)}, f32[2048,128]{1,0:T(8,128)S(1)}, u32[]{:S(2)}, u32[]{:S(2)}) %collective-permute-start.8) | collective-permute-done | bytes 1048608 | tf_op jit(solution)/shard_map/ppermute | solution.py:399
  89.5 23.7 %collective-permute-done.9.refs_5_ = f32[2048,128]{1,0:T(8,128)S(1)} collective-permute-done((f32[2048,128]{1,0:T(8,128)S(1)}, f32[2048,128]{1,0:T(8,128)S(1)}, u32[]{:S(2)}, u32[]{:S(2)}) %collective-permute-start.9) | collective-permute-done | bytes 1048608 | tf_op jit(solution)/shard_map/ppermute | solution.py:399
  113.3 21.6 %collective-permute-done.10.refs_6_ = f32[2048,128]{1,0:T(8,128)S(1)} collective-permute-done((f32[2048,128]{1,0:T(8,128)S(1)}, f32[2048,128]{1,0:T(8,128)S(1)}, u32[]{:S(2)}, u32[]{:S(2)}) %collective-permute-start.10) | collective-permute-done | bytes 1048608 | tf_op jit(solution)/shard_map/ppermute | solution.py:399
  134.9 6.4 %finish.1 = (f32[8192,128]{1,0:T(8,128)}, f32[2048,128]{1,0:T(8,128)}, f32[512,128]{1,0:T(8,128)}, f32[40,128]{1,0:T(8,128)S(1)}, f32[40,128]{1,0:T(8,128)S(1)},...) custom-call(s32[2]{0:T(128)S(1)} %pad_add_fusion.me_ref, s32[64,1,324]{2,1,0:T(1,128)} %constant.14.clone.take_ref, ...), custom_call_target="tpu_custom_call" | custom-call | tf_op jit(solution)/shard_map/finish/pallas_call | solution.py:320
  141.3 1.7 %collective-permute-start.17 = (f32[40,128]{1,0:T(8,128)S(1)}, f32[40,128]{1,0:T(8,128)S(1)}, u32[]{:S(2)}, u32[]{:S(2)}) collective-permute-start(f32[40,128]{1,0:T(8,128)S(1)} %get-tuple-element.44), channel_id=1, source_target_pairs={{0,1},{1,2},{2,3},{3,0},{4,5},{5,6},{6,7},{7,4},{8,9},{9,10},{10,1... | collective-permute-start | bytes 61448 | tf_op jit(solution)/shard_map/ppermute | solution.py:403
  143.0 2.9 %collective-permute-start.18 = (f32[40,128]{1,0:T(8,128)S(1)}, f32[40,128]{1,0:T(8,128)S(1)}, u32[]{:S(2)}, u32[]{:S(2)}) collective-permute-start(f32[40,128]{1,0:T(8,128)S(1)} %get-tuple-element.45), channel_id=1, source_target_pairs={{0,2},{1,3},{2,0},{3,1},{4,6},{5,7},{6,4},{7,5},{8,10},{9,11},{10,... | collective-permute-start | bytes 61448 | tf_op jit(solution)/shard_map/ppermute | solution.py:403
  145.9 1.3 collective-permute-start.19
  148.3 1.4 collective-permute-done.19.refs_3_
  149.7 1.2 join.1
  (23 shorter events, 6.8 us)
Async XLA Ops:
  0.7 2.2 %copy-start = (f32[128,8192]{1,0:T(8,128)S(1)}, f32[128,8192]{1,0:T(8,128)}, u32[]{:S(2)}) copy-start(f32[128,8192]{1,0:T(8,128)} %param.5) | copy-start | bytes 12582916
  5.2 41.1 %collective-permute-start.4 = (f32[1024,128]{1,0:T(8,128)S(1)}, f32[1024,128]{1,0:T(8,128)S(1)}, u32[]{:S(2)}, u32[]{:S(2)}) collective-permute-start(f32[1024,128]{1,0:T(8,128)S(1)} %get-tuple-element.29), channel_id=1, source_target_pairs={{28,244},{52,12},{164,156},{168,128},{172,132},{200,160},{212,172}... | collective-permute-start | bytes 1572872 | tf_op jit(solution)/shard_map/ppermute | solution.py:399
  11.7 20.2 %collective-permute-start.14 = (f32[512,128]{1,0:T(8,128)S(1)}, f32[512,128]{1,0:T(8,128)S(1)}, u32[]{:S(2)}, u32[]{:S(2)}) collective-permute-start(f32[512,128]{1,0:T(8,128)S(1)} %get-tuple-element.37), channel_id=1, source_target_pairs={{0,0},{8,12},{12,20},{16,28},{20,36},{24,40},{28,44},{32,56},{36,6... | collective-permute-start | bytes 786440 | tf_op jit(solution)/shard_map/ppermute | solution.py:399
  14.5 30.4 %collective-permute-start.15 = (f32[512,128]{1,0:T(8,128)S(1)}, f32[512,128]{1,0:T(8,128)S(1)}, u32[]{:S(2)}, u32[]{:S(2)}) collective-permute-start(f32[512,128]{1,0:T(8,128)S(1)} %get-tuple-element.38), channel_id=1, source_target_pairs={{0,4},{4,12},{12,20},{16,28},{20,36},{24,44},{28,52},{36,56},{40,6... | collective-permute-start | bytes 786440 | tf_op jit(solution)/shard_map/ppermute | solution.py:399
  16.6 29.0 %collective-permute-start.16 = (f32[512,128]{1,0:T(8,128)S(1)}, f32[512,128]{1,0:T(8,128)S(1)}, u32[]{:S(2)}, u32[]{:S(2)}) collective-permute-start(f32[512,128]{1,0:T(8,128)S(1)} %get-tuple-element.39), channel_id=1, source_target_pairs={{0,4},{8,20},{12,24},{20,36},{32,56},{40,68},{52,76},{56,88},{76,1... | collective-permute-start | bytes 786440 | tf_op jit(solution)/shard_map/ppermute | solution.py:399
  17.3 31.0 %collective-permute-start.6 = (f32[1024,128]{1,0:T(8,128)S(1)}, f32[1024,128]{1,0:T(8,128)S(1)}, u32[]{:S(2)}, u32[]{:S(2)}) collective-permute-start(f32[1024,128]{1,0:T(8,128)S(1)} %get-tuple-element.30), channel_id=1, source_target_pairs={{192,248},{200,224},{204,228},{193,249},{201,225},{205,229},{194,2... | collective-permute-start | bytes 1572872 | tf_op jit(solution)/shard_map/ppermute | solution.py:399
  31.9 17.0 %collective-permute-start.11 = (f32[1024,128]{1,0:T(8,128)S(1)}, f32[1024,128]{1,0:T(8,128)S(1)}, u32[]{:S(2)}, u32[]{:S(2)}) collective-permute-start(f32[1024,128]{1,0:T(8,128)S(1)} %get-tuple-element.34), channel_id=1, source_target_pairs={{4,4},{8,12},{12,24},{16,28},{20,36},{24,40},{28,48},{32,52},{36,5... | collective-permute-start | bytes 1572872 | tf_op jit(solution)/shard_map/ppermute | solution.py:399
  44.8 18.3 %collective-permute-start = (f32[2048,128]{1,0:T(8,128)S(1)}, f32[2048,128]{1,0:T(8,128)S(1)}, u32[]{:S(2)}, u32[]{:S(2)}) collective-permute-start(f32[2048,128]{1,0:T(8,128)S(1)} %get-tuple-element.27), channel_id=1, source_target_pairs={{24,0},{60,36},{88,64},{168,176},{188,164},{216,192},{25,1},{61,37... | collective-permute-start | bytes 3145736 | tf_op jit(solution)/shard_map/ppermute | solution.py:399
  45.6 29.3 %collective-permute-start.2 = (f32[2048,128]{1,0:T(8,128)S(1)}, f32[2048,128]{1,0:T(8,128)S(1)}, u32[]{:S(2)}, u32[]{:S(2)}) collective-permute-start(f32[2048,128]{1,0:T(8,128)S(1)} %get-tuple-element.28), channel_id=1, source_target_pairs={{40,32},{44,36},{52,44},{168,160},{41,33},{45,37},{53,45},{169,161... | collective-permute-start | bytes 3145736 | tf_op jit(solution)/shard_map/ppermute | solution.py:399
  46.3 13.5 %collective-permute-start.12 = (f32[1024,128]{1,0:T(8,128)S(1)}, f32[1024,128]{1,0:T(8,128)S(1)}, u32[]{:S(2)}, u32[]{:S(2)}) collective-permute-start(f32[1024,128]{1,0:T(8,128)S(1)} %get-tuple-element.35), channel_id=1, source_target_pairs={{0,4},{4,8},{8,16},{16,28},{20,36},{24,40},{28,48},{36,56},{44,68}... | collective-permute-start | bytes 1572872 | tf_op jit(solution)/shard_map/ppermute | solution.py:399
  48.2 12.2 %collective-permute-start.13 = (f32[1024,128]{1,0:T(8,128)S(1)}, f32[1024,128]{1,0:T(8,128)S(1)}, u32[]{:S(2)}, u32[]{:S(2)}) collective-permute-start(f32[1024,128]{1,0:T(8,128)S(1)} %get-tuple-element.36), channel_id=1, source_target_pairs={{4,12},{12,28},{28,52},{32,56},{48,72},{60,92},{68,100},{76,108},{... | collective-permute-start | bytes 1572872 | tf_op jit(solution)/shard_map/ppermute | solution.py:399
  49.0 12.8 %collective-permute-start.5 = (f32[1024,128]{1,0:T(8,128)S(1)}, f32[1024,128]{1,0:T(8,128)S(1)}, u32[]{:S(2)}, u32[]{:S(2)}) collective-permute-start(f32[1024,128]{1,0:T(8,128)S(1)} %collective-permute-done.4), channel_id=1, source_target_pairs={{244,44},{12,80},{156,188},{128,192},{132,196},{160,216},{172,224}... | collective-permute-start | bytes 1572872 | tf_op jit(solution)/shard_map/ppermute | solution.py:399
  59.8 15.8 %collective-permute-start.7 = (f32[1024,128]{1,0:T(8,128)S(1)}, f32[1024,128]{1,0:T(8,128)S(1)}, u32[]{:S(2)}, u32[]{:S(2)}) collective-permute-start(f32[1024,128]{1,0:T(8,128)S(1)} %collective-permute-done.6), channel_id=1, source_target_pairs={{248,208},{224,216},{228,220},{249,209},{225,217},{229,221},{250,2... | collective-permute-start | bytes 1572872 | tf_op jit(solution)/shard_map/ppermute | solution.py:399
  60.5 29.0 %collective-permute-start.8 = (f32[2048,128]{1,0:T(8,128)S(1)}, f32[2048,128]{1,0:T(8,128)S(1)}, u32[]{:S(2)}, u32[]{:S(2)}) collective-permute-start(f32[2048,128]{1,0:T(8,128)S(1)} %get-tuple-element.31), channel_id=1, source_target_pairs={{0,0},{4,8},{8,16},{12,20},{16,28},{20,32},{24,44},{28,48},{32,52}... | collective-permute-start | bytes 3145736 | tf_op jit(solution)/shard_map/ppermute | solution.py:399
  61.8 51.5 %collective-permute-start.9 = (f32[2048,128]{1,0:T(8,128)S(1)}, f32[2048,128]{1,0:T(8,128)S(1)}, u32[]{:S(2)}, u32[]{:S(2)}) collective-permute-start(f32[2048,128]{1,0:T(8,128)S(1)} %get-tuple-element.32), channel_id=1, source_target_pairs={{0,0},{4,8},{8,16},{12,24},{16,32},{20,36},{24,44},{28,48},{32,52}... | collective-permute-start | bytes 3145736 | tf_op jit(solution)/shard_map/ppermute | solution.py:399
  63.1 71.8 %collective-permute-start.10 = (f32[2048,128]{1,0:T(8,128)S(1)}, f32[2048,128]{1,0:T(8,128)S(1)}, u32[]{:S(2)}, u32[]{:S(2)}) collective-permute-start(f32[2048,128]{1,0:T(8,128)S(1)} %get-tuple-element.33), channel_id=1, source_target_pairs={{0,4},{4,12},{8,20},{12,24},{16,32},{20,40},{32,56},{36,60},{40,68... | collective-permute-start | bytes 3145736 | tf_op jit(solution)/shard_map/ppermute | solution.py:399
  74.9 60.0 %collective-permute-start.1 = (f32[2048,128]{1,0:T(8,128)S(1)}, f32[2048,128]{1,0:T(8,128)S(1)}, u32[]{:S(2)}, u32[]{:S(2)}) collective-permute-start(f32[2048,128]{1,0:T(8,128)S(1)} %collective-permute-done), channel_id=1, source_target_pairs={{0,40},{36,92},{64,120},{176,188},{164,204},{192,228},{1,41},{37,9... | collective-permute-start | bytes 3145736 | tf_op jit(solution)/shard_map/ppermute | solution.py:399
  75.6 59.3 %collective-permute-start.3 = (f32[2048,128]{1,0:T(8,128)S(1)}, f32[2048,128]{1,0:T(8,128)S(1)}, u32[]{:S(2)}, u32[]{:S(2)}) collective-permute-start(f32[2048,128]{1,0:T(8,128)S(1)} %collective-permute-done.2), channel_id=1, source_target_pairs={{32,64},{36,68},{44,80},{160,192},{33,65},{37,69},{45,81},{161,193... | collective-permute-start | bytes 3145736 | tf_op jit(solution)/shard_map/ppermute | solution.py:399
  141.3 5.9 %collective-permute-start.17 = (f32[40,128]{1,0:T(8,128)S(1)}, f32[40,128]{1,0:T(8,128)S(1)}, u32[]{:S(2)}, u32[]{:S(2)}) collective-permute-start(f32[40,128]{1,0:T(8,128)S(1)} %get-tuple-element.44), channel_id=1, source_target_pairs={{0,1},{1,2},{2,3},{3,0},{4,5},{5,6},{6,7},{7,4},{8,9},{9,10},{10,1... | collective-permute-start | bytes 61448 | tf_op jit(solution)/shard_map/ppermute | solution.py:403
  143.0 5.3 %collective-permute-start.18 = (f32[40,128]{1,0:T(8,128)S(1)}, f32[40,128]{1,0:T(8,128)S(1)}, u32[]{:S(2)}, u32[]{:S(2)}) collective-permute-start(f32[40,128]{1,0:T(8,128)S(1)} %get-tuple-element.45), channel_id=1, source_target_pairs={{0,2},{1,3},{2,0},{3,1},{4,6},{5,7},{6,4},{7,5},{8,10},{9,11},{10,... | collective-permute-start | bytes 61448 | tf_op jit(solution)/shard_map/ppermute | solution.py:403
  145.9 3.8 %collective-permute-start.19 = (f32[40,128]{1,0:T(8,128)S(1)}, f32[40,128]{1,0:T(8,128)S(1)}, u32[]{:S(2)}, u32[]{:S(2)}) collective-permute-start(f32[40,128]{1,0:T(8,128)S(1)} %get-tuple-element.46), channel_id=1, source_target_pairs={{0,3},{1,0},{2,1},{3,2},{4,7},{5,4},{6,5},{7,6},{8,11},{9,8},{10,9... | collective-permute-start | bytes 61448 | tf_op jit(solution)/shard_map/ppermute | solution.py:403
where the time goes:
time: 151 us
  waiting for transfers between devices  93.5 us (62%)
  starting transfers between devices  40.4 us (27%)
  Pallas kernels  13.9 us (9%)
  local copies, waits for them, and re-layouts  2.19 us (1%)
    ppermute x17, waiting for transfers between devices, body(): blocks[j].append(lax.ppermute(blocks[j][-1], 'rows', tracks[j][i]))  91.1 us
    ppermute x17, starting transfers between devices, body(): blocks[j].append(lax.ppermute(blocks[j][-1], 'rows', tracks[j][i]))  34.5 us
    pallas_call x1, Pallas kernels, finish(): pl.pallas_call(kernel, grid_spec=pltpu.PrefetchScalarGridSpec(num_scalar_...  6.42 us
    pallas_call x2, Pallas kernels, pack_rows(): pl.pallas_call(kernel, grid_spec=pltpu.PrefetchScalarGridSpec(num_scalar_...  6.2 us
    ppermute x3, starting transfers between devices, body(): lax.ppermute(smalls[k], 'cols', [(c, (c + k) % 4) for c in range(4)])  5.91 us
  transfers between devices with their start and end apart: 20, of which 8 were waited for; matrix products, arithmetic and copies ran while one was open for 0% of the time, Pallas kernels for 3%

commit v1 on v0

--- a/solution.py
+++ b/solution.py
@@ -12,8 +12,8 @@
 TOTAL = 8192
 ROWS = 64
 OWN = TOTAL // ROWS
-SLOTS = (9, 10, 11, 12, 0, 1, 2, 3, 4, 5, 6, 7, 8)
-ISSUE = (0, 2, 4, 6, 8, 10, 12, 14, 16, 18, 20, 22, 24, 1, 3, 5, 7)
+SLOTS = (13, 6, 9, 3, 12, 11, 7, 10, 4, 0, 1, 2, 14, 5, 8)
+ISSUE = (0, 2, 4, 6, 8, 10, 12, 14, 16, 18, 20, 22, 24, 11, 5, 9, 1, 26, 25, 15, 28)
 SPAN = 3
 CODE = 1024
 
@@ -21,34 +21,38 @@
     "D": (),
     "P": ((0, 1),),
     "M": ((0, -1),),
+    "N": ((-4, 0),),
+    "O": ((-3, 0),),
     "V": ((1, -1),),
     "Y": ((-1, -1),),
 }
-CLASSES = (("D", 32, 3), ("D", 16, 3), ("D", 8, 3), ("P", 32, 1), ("M", 32, 1), ("Y", 16, 1), ("V", 16, 1))
+CLASSES = (("D", 32, 3), ("D", 16, 3), ("D", 8, 3), ("P", 32, 1), ("M", 32, 1), ("Y", 16, 1), ("V", 16, 1), ("N", 24, 1), ("O", 24, 1))
 ROUTES = (
-    2, 65, 513, 545, 578, 33313, 33794, 33825, 34305, 34337, 34369, 67105,
-    67137, 67586, 67617, 68097, 68161, 100865, 100930, 101378, 101409, 101441, 101921, 134657,
-    134690, 134722, 135170, 167937, 168449, 168482, 168515, 168961, 201762, 201793, 201825, 202242,
-    202305, 235073, 235169, 235522, 235554, 236065, 236097, 268802, 268833, 269313, 269345, 269378,
-    302114, 302145, 302595, 303169, 335425, 335874, 335937, 336001, 336385, 336449, 369186, 369217,
-    369281, 369666, 402467, 402947, 435779, 436226, 436353, 436385, 436769, 469507, 469569, 470049,
-    470082, 502786, 502817, 502849, 503329, 503361, 503393, 536065, 536098, 536129, 536578, 536641,
-    569345, 569377, 569409, 569858, 569889, 569921, 602658, 602689, 603139, 635937, 635970, 636418,
-    636450, 636481, 669217, 669249, 669698, 669730, 669762, 702497, 702979, 703043, 735777, 736258,
-    736290, 736353, 769090, 769539, 769570, 802370, 802819, 802849, 802881, 835617, 836098, 836130,
-    836162, 868897, 868929, 869378, 869410, 869442, 902145, 902657, 902691, 902722, 935425, 935489,
-    935938, 935969, 936001, 968705, 968737, 969217, 969250, 969282, 1001986, 1002497, 1002529, 1002562,
-    1035266, 1035297, 1035777, 1035842, 1068546, 1068578, 1069057, 1101826, 1101859, 1102402, 1135107, 1135137,
-    1135169, 1167905, 1168386, 1168418, 1168449, 1201153, 1201217, 1201665, 1201699, 1234434, 1234945, 1234977,
-    1235009, 1267714, 1267745, 1267777, 1268258, 1300995, 1301025, 1301569, 1333825, 1334275, 1334338, 1367074,
-    1367554, 1367713, 1400353, 1400385, 1400417, 1400897, 1400961, 1400993, 1433601, 1433635, 1433665, 1434177,
-    1434273, 1466883, 1466913, 1499681, 1500163, 1532962, 1532993, 1533442, 1566209, 1566273, 1566305, 1566721,
-    1566785, 1599490, 1599521, 1599553, 1599681, 1632321, 1632771, 1632833, 1665570, 1665601, 1666049, 1666113,
-    1666209, 1666241, 1698818, 1698881, 1699361, 1699393, 1699521, 1732098, 1732130, 1732161, 1764929, 1765378,
-    1765409, 1765537, 1798178, 1798209, 1798657, 1798753, 1831426, 1831457, 1831969, 1832002, 1864707, 1864769,
-    1897505, 1897986, 1898017, 1898049, 1930753, 1930785, 1930817, 1931265, 1931297, 1931329, 1964034, 1964065,
-    1964097, 1964610, 1997314, 1997346, 1997377, 2030081, 2030593, 2030626, 2030658, 2063362, 2063873, 2063937,
-    2096642, 2096674,
+    1632961, 503297, 1068547, 836321, 736259, 1268225, 1135139, 1500161, 1466977, 1400866, 1532993, 1964034,
+    1997314, 1069090, 369313, 1964610, 536577, 1533025, 536066, 1732098, 1997377, 2063394, 369377, 336385,
+    1101889, 969249, 1599523, 1533506, 1599681, 134689, 1135169, 335425, 1334433, 302594, 969281, 1035841,
+    469601, 1665570, 1665601, 702497, 968770, 1267714, 502785, 1666209, 269346, 436449, 1002018, 67137,
+    1566273, 2030081, 1234945, 569922, 302145, 502817, 135202, 33825, 201761, 1500289, 669249, 1798145,
+    603201, 1698850, 1764929, 836098, 1400385, 202241, 1267745, 168994, 1002497, 1964065, 802850, 1798209,
+    1001985, 1732161, 1234498, 1931297, 1035809, 503329, 1434177, 868897, 868929, 2063939, 236097, 602625,
+    1599553, 1831426, 403073, 836129, 1466913, 1201153, 469537, 669729, 436226, 469505, 669698, 1101857,
+    1367074, 1300994, 469571, 269313, 669953, 1135233, 545, 1698881, 67105, 502881, 968738, 1897505,
+    68097, 436257, 1897986, 1102402, 669217, 1135105, 135169, 168577, 435777, 369730, 1400897, 1168033,
+    569409, 703042, 303169, 1002561, 336001, 1599489, 1765378, 1566721, 335907, 67586, 1035330, 34305,
+    168481, 578, 869441, 235041, 536833, 1798657, 1566785, 1699489, 68161, 101441, 2, 1930753,
+    1201217, 101921, 236065, 603138, 1666049, 1168449, 536129, 902881, 869409, 402978, 435745, 1898017,
+    935489, 1367745, 1168418, 570113, 1632833, 1234465, 636418, 769538, 702978, 1831970, 235522, 736513,
+    101378, 902658, 802337, 201793, 869378, 1333825, 1931265, 101409, 902145, 1765569, 369697, 168513,
+    1931329, 769793, 569857, 736321, 513, 100897, 302626, 1732130, 1400353, 1301121, 2030625, 201889,
+    335937, 935425, 1433601, 1400993, 1864769, 1235201, 34369, 1798753, 1466882, 636482, 2096643, 1201697,
+    436769, 536609, 836161, 803041, 369153, 1930785, 34337, 202274, 503361, 769090, 1301025, 703009,
+    669761, 403009, 302081, 235073, 336033, 268866, 167937, 569889, 636673, 33794, 869601, 1533475,
+    769633, 403169, 1434273, 635905, 168449, 1334275, 603393, 1500194, 1002721, 569377, 1666113, 1632770,
+    1997346, 936161, 1632321, 1765537, 902721, 1035266, 100865, 2030594, 1699393, 602689, 33313, 502849,
+    1102081, 1433665, 268802, 1499681, 1964097, 1433633, 235617, 769601, 1566210, 1898049, 470017, 336449,
+    1666241, 1234561, 1831457, 569345, 1301569, 1699521, 2063905, 402465, 1267777, 2063361, 65, 802818,
+    703233, 1367554, 1864707, 935938, 735777, 1930817, 835617, 969217, 67617, 1168386, 436289, 1201666,
+    1433729, 402433, 969441, 1400417, 1632801, 1698817, 201825, 1101826, 369793, 1036001, 134658, 202305,
 )
 
 

time: 151 us -> 171 us (1.13)
  the two profiles are of different devices: /device:TPU:194 before, /device:TPU:96 now
where the time goes in v1:
time: 171 us; the launch traced here: 170 us
  waiting for transfers between devices  112 us (65%)
  starting transfers between devices  40.3 us (24%)
  Pallas kernels  14.4 us (8%)
  local copies, waits for them, and re-layouts  2.19 us (1%)
    ppermute x21, waiting for transfers between devices, body(): blocks[j].append(lax.ppermute(blocks[j][-1], 'rows', tracks[j][i]))  110 us
    ppermute x21, starting transfers between devices, body(): blocks[j].append(lax.ppermute(blocks[j][-1], 'rows', tracks[j][i]))  34.4 us
    pallas_call x2, Pallas kernels, pack_rows(): pl.pallas_call(kernel, grid_spec=pltpu.PrefetchScalarGridSpec(num_scalar_...  6.7 us
    pallas_call x1, Pallas kernels, finish(): pl.pallas_call(kernel, grid_spec=pltpu.PrefetchScalarGridSpec(num_scalar_...  6.5 us
    ppermute x3, starting transfers between devices, body(): lax.ppermute(smalls[k], 'cols', [(c, (c + k) % 4) for c in range(4)])  5.9 us
  transfers between devices with their start and end apart: 24, of which 8 were waited for; matrix products, arithmetic and copies ran while one was open for 0% of the time, Pallas kernels for 2%

profile of v1, /device:TPU:96, one launch (start us, length us, event | category | flops | bytes accessed | tf_op | source)
XLA Modules:
  0.0 170.4 jit_solution(5979865228981710906)
XLA Ops:
  0.7 2.2 %copy-done = f32[128,8192]{1,0:T(8,128)S(1)} copy-done((f32[128,8192]{1,0:T(8,128)S(1)}, f32[128,8192]{1,0:T(8,128)}, u32[]{:S(2)}) %copy-start) | copy-done | bytes 4194328
  2.9 2.5 %pack_rows.2 = (f32[1536,128]{1,0:T(8,128)S(1)}, f32[512,128]{1,0:T(8,128)S(1)}, f32[2048,128]{1,0:T(8,128)S(1)}) custom-call(s32[2]{0:T(128)S(1)} %pad_add_fusion.me_ref, s32[64,1,328]{2,1,0:T(1,128)} %constant.13.clone.send_ref, s32[64,1,128]{2,1,0:T(1,128)} %bitcast.26, f32[64,1,128]{2,1,0:T(1,128)} %bitcast.29, f32[8192,128]{1,0:T(8,128)S(1)} %bitcast.24), custom_call_target="tpu_custom_call" | custom-call | tf_op jit(solution)/shard_map/pack_rows/pallas_call | solution.py:211
  6.0 4.2 %pack_rows.3 = (f32[1024,128]{1,0:T(8,128)S(1)}, f32[1024,128]{1,0:T(8,128)S(1)}, f32[1024,128]{1,0:T(8,128)S(1)}, f32[512,128]{1,0:T(8,128)S(1)}, f32[2048,128]...) custom-call(s32[2]{0:T(128)S(1)} %pad_add_fusion.me_ref, ...), custom_call_target="tpu_custom_call" | custom-call | tf_op jit(solution)/shard_map/pack_rows/pallas_call | solution.py:211
  10.3 4.9 %collective-permute-start.5 = (f32[1024,128]{1,0:T(8,128)S(1)}, f32[1024,128]{1,0:T(8,128)S(1)}, u32[]{:S(2)}, u32[]{:S(2)}) collective-permute-start(f32[1024,128]{1,0:T(8,128)S(1)} %get-tuple-element.32), channel_id=1, source_target_pairs={{0,4},{4,8},{8,12},{12,28},{16,32},{20,40},{24,44},{28,52},{32,56}... | collective-permute-start | bytes 1572872 | tf_op jit(solution)/shard_map/ppermute | solution.py:403
  15.2 1.3 collective-permute-start.10
  18.6 11.2 %collective-permute-done.10.refs_6_ = f32[512,128]{1,0:T(8,128)S(1)} collective-permute-done((f32[512,128]{1,0:T(8,128)S(1)}, f32[512,128]{1,0:T(8,128)S(1)}, u32[]{:S(2)}, u32[]{:S(2)}) %collective-permute-start.10) | collective-permute-done | bytes 262176 | tf_op jit(solution)/shard_map/ppermute | solution.py:403
  29.8 1.3 collective-permute-start
  31.9 7.8 %collective-permute-start.13 = (f32[1024,128]{1,0:T(8,128)S(1)}, f32[1024,128]{1,0:T(8,128)S(1)}, u32[]{:S(2)}, u32[]{:S(2)}) collective-permute-start(f32[1024,128]{1,0:T(8,128)S(1)} %get-tuple-element.37), channel_id=1, source_target_pairs={{4,12},{8,16},{12,24},{16,28},{20,40},{24,44},{32,56},{36,60},{40,... | collective-permute-start | bytes 1572872 | tf_op jit(solution)/shard_map/ppermute | solution.py:403
  39.7 1.3 collective-permute-start.19
  41.8 5.3 %collective-permute-done.13.refs_8_ = f32[1024,128]{1,0:T(8,128)S(1)} collective-permute-done((f32[1024,128]{1,0:T(8,128)S(1)}, f32[1024,128]{1,0:T(8,128)S(1)}, u32[]{:S(2)}, u32[]{:S(2)}) %collective-permute-start.13) | collective-permute-done | bytes 524320 | tf_op jit(solution)/shard_map/ppermute | solution.py:403
  47.9 5.4 %collective-permute-start.14 = (f32[2048,128]{1,0:T(8,128)S(1)}, f32[2048,128]{1,0:T(8,128)S(1)}, u32[]{:S(2)}, u32[]{:S(2)}) collective-permute-start(f32[2048,128]{1,0:T(8,128)S(1)} %get-tuple-element.38), channel_id=1, source_target_pairs={{0,0},{4,12},{8,20},{12,24},{16,28},{20,32},{24,44},{28,48},{32,56... | collective-permute-start | bytes 3145736 | tf_op jit(solution)/shard_map/ppermute | solution.py:403
  53.3 3.1 %collective-permute-done = f32[1536,128]{1,0:T(8,128)S(1)} collective-permute-done((f32[1536,128]{1,0:T(8,128)S(1)}, f32[1536,128]{1,0:T(8,128)S(1)}, u32[]{:S(2)}, u32[]{:S(2)}) %collective-permute-start) | collective-permute-done | bytes 786464 | tf_op jit(solution)/shard_map/ppermute | solution.py:403
  56.4 1.9 %collective-permute-start.15 = (f32[2048,128]{1,0:T(8,128)S(1)}, f32[2048,128]{1,0:T(8,128)S(1)}, u32[]{:S(2)}, u32[]{:S(2)}) collective-permute-start(f32[2048,128]{1,0:T(8,128)S(1)} %get-tuple-element.39), channel_id=1, source_target_pairs={{0,0},{4,8},{8,16},{12,24},{16,32},{20,36},{28,48},{32,52},{36,60}... | collective-permute-start | bytes 3145736 | tf_op jit(solution)/shard_map/ppermute | solution.py:403
  61.9 16.6 %collective-permute-done.14.refs_9_ = f32[2048,128]{1,0:T(8,128)S(1)} collective-permute-done((f32[2048,128]{1,0:T(8,128)S(1)}, f32[2048,128]{1,0:T(8,128)S(1)}, u32[]{:S(2)}, u32[]{:S(2)}) %collective-permute-start.14) | collective-permute-done | bytes 1048608 | tf_op jit(solution)/shard_map/ppermute | solution.py:403
  79.3 20.0 %collective-permute-done.15.refs_10_ = f32[2048,128]{1,0:T(8,128)S(1)} collective-permute-done((f32[2048,128]{1,0:T(8,128)S(1)}, f32[2048,128]{1,0:T(8,128)S(1)}, u32[]{:S(2)}, u32[]{:S(2)}) %collective-permute-start.15) | collective-permute-done | bytes 1048608 | tf_op jit(solution)/shard_map/ppermute | solution.py:403
  99.3 1.3 collective-permute-start.18
  100.6 53.7 %collective-permute-done.18.refs_12_ = f32[1536,128]{1,0:T(8,128)S(1)} collective-permute-done((f32[1536,128]{1,0:T(8,128)S(1)}, f32[1536,128]{1,0:T(8,128)S(1)}, u32[]{:S(2)}, u32[]{:S(2)}) %collective-permute-start.18) | collective-permute-done | bytes 786464 | tf_op jit(solution)/shard_map/ppermute | solution.py:403
  154.3 6.5 %finish.1 = (f32[8192,128]{1,0:T(8,128)}, f32[2048,128]{1,0:T(8,128)}, f32[512,128]{1,0:T(8,128)}, f32[40,128]{1,0:T(8,128)S(1)}, f32[40,128]{1,0:T(8,128)S(1)},...) custom-call(s32[2]{0:T(128)S(1)} %pad_add_fusion.me_ref, s32[64,1,326]{2,1,0:T(1,128)} %constant.14.clone.take_ref, ...), custom_call_target="tpu_custom_call" | custom-call | tf_op jit(solution)/shard_map/finish/pallas_call | solution.py:324
  160.8 1.6 collective-permute-start.21
  162.5 2.9 %collective-permute-start.22 = (f32[40,128]{1,0:T(8,128)S(1)}, f32[40,128]{1,0:T(8,128)S(1)}, u32[]{:S(2)}, u32[]{:S(2)}) collective-permute-start(f32[40,128]{1,0:T(8,128)S(1)} %get-tuple-element.49), channel_id=1, source_target_pairs={{0,2},{1,3},{2,0},{3,1},{4,6},{5,7},{6,4},{7,5},{8,10},{9,11},{10,... | collective-permute-start | bytes 61448 | tf_op jit(solution)/shard_map/ppermute | solution.py:407
  165.4 1.3 collective-permute-start.23
  166.7 1.0 collective-permute-done.22.refs_2_
  167.8 1.4 collective-permute-done.23.refs_3_
  169.2 1.2 join.1
  (31 shorter events, 9.3 us)
Async XLA Ops:
  5.4 12.5 %collective-permute-start.2 = (f32[512,128]{1,0:T(8,128)S(1)}, f32[512,128]{1,0:T(8,128)S(1)}, u32[]{:S(2)}, u32[]{:S(2)}) collective-permute-start(f32[512,128]{1,0:T(8,128)S(1)} %get-tuple-element.30), channel_id=1, source_target_pairs={{0,4},{4,12},{8,20},{12,24},{20,36},{24,40},{28,44},{32,52},{36,64... | collective-permute-start | bytes 786440 | tf_op jit(solution)/shard_map/ppermute | solution.py:403
  10.3 21.6 %collective-permute-start.5 = (f32[1024,128]{1,0:T(8,128)S(1)}, f32[1024,128]{1,0:T(8,128)S(1)}, u32[]{:S(2)}, u32[]{:S(2)}) collective-permute-start(f32[1024,128]{1,0:T(8,128)S(1)} %get-tuple-element.32), channel_id=1, source_target_pairs={{0,4},{4,8},{8,12},{12,28},{16,32},{20,40},{24,44},{28,52},{32,56}... | collective-permute-start | bytes 1572872 | tf_op jit(solution)/shard_map/ppermute | solution.py:403
  15.2 14.6 %collective-permute-start.10 = (f32[512,128]{1,0:T(8,128)S(1)}, f32[512,128]{1,0:T(8,128)S(1)}, u32[]{:S(2)}, u32[]{:S(2)}) collective-permute-start(f32[512,128]{1,0:T(8,128)S(1)} %get-tuple-element.35), channel_id=1, source_target_pairs={{0,4},{8,12},{24,44},{32,52},{36,56},{40,64},{44,72},{52,76},{56,8... | collective-permute-start | bytes 786440 | tf_op jit(solution)/shard_map/ppermute | solution.py:403
  16.5 23.2 %collective-permute-start.6 = (f32[1024,128]{1,0:T(8,128)S(1)}, f32[1024,128]{1,0:T(8,128)S(1)}, u32[]{:S(2)}, u32[]{:S(2)}) collective-permute-start(f32[1024,128]{1,0:T(8,128)S(1)} %get-tuple-element.33), channel_id=1, source_target_pairs={{164,220},{192,248},{196,252},{200,224},{204,228},{212,236},{165,2... | collective-permute-start | bytes 1572872 | tf_op jit(solution)/shard_map/ppermute | solution.py:403
  17.2 23.9 %collective-permute-start.8 = (f32[1024,128]{1,0:T(8,128)S(1)}, f32[1024,128]{1,0:T(8,128)S(1)}, u32[]{:S(2)}, u32[]{:S(2)}) collective-permute-start(f32[1024,128]{1,0:T(8,128)S(1)} %get-tuple-element.34), channel_id=1, source_target_pairs={{24,240},{40,0},{44,4},{140,100},{160,152},{168,128},{172,132},{20... | collective-permute-start | bytes 1572872 | tf_op jit(solution)/shard_map/ppermute | solution.py:403
  17.9 13.2 %collective-permute-start.20 = (f32[512,128]{1,0:T(8,128)S(1)}, f32[512,128]{1,0:T(8,128)S(1)}, u32[]{:S(2)}, u32[]{:S(2)}) collective-permute-start(f32[512,128]{1,0:T(8,128)S(1)} %get-tuple-element.43), channel_id=1, source_target_pairs={{0,0},{28,52},{40,68},{56,84},{68,100},{80,108},{88,120},{92,124},... | collective-permute-start | bytes 786440 | tf_op jit(solution)/shard_map/ppermute | solution.py:403
  29.8 26.6 %collective-permute-start = (f32[1536,128]{1,0:T(8,128)S(1)}, f32[1536,128]{1,0:T(8,128)S(1)}, u32[]{:S(2)}, u32[]{:S(2)}) collective-permute-start(f32[1536,128]{1,0:T(8,128)S(1)} %get-tuple-element.29), channel_id=1, source_target_pairs={{44,172},{48,176},{52,180},{96,224},{100,228},{104,232},{108,236},... | collective-permute-start | bytes 2359304 | tf_op jit(solution)/shard_map/ppermute | solution.py:403
  31.1 27.8 %collective-permute-start.3 = (f32[2048,128]{1,0:T(8,128)S(1)}, f32[2048,128]{1,0:T(8,128)S(1)}, u32[]{:S(2)}, u32[]{:S(2)}) collective-permute-start(f32[2048,128]{1,0:T(8,128)S(1)} %get-tuple-element.31), channel_id=1, source_target_pairs={{24,0},{28,4},{56,32},{60,36},{92,68},{168,176},{176,184},{184,160... | collective-permute-start | bytes 3145736 | tf_op jit(solution)/shard_map/ppermute | solution.py:403
  31.9 15.2 %collective-permute-start.13 = (f32[1024,128]{1,0:T(8,128)S(1)}, f32[1024,128]{1,0:T(8,128)S(1)}, u32[]{:S(2)}, u32[]{:S(2)}) collective-permute-start(f32[1024,128]{1,0:T(8,128)S(1)} %get-tuple-element.37), channel_id=1, source_target_pairs={{4,12},{8,16},{12,24},{16,28},{20,40},{24,44},{32,56},{36,60},{40,... | collective-permute-start | bytes 1572872 | tf_op jit(solution)/shard_map/ppermute | solution.py:403
  39.7 8.1 %collective-permute-start.19 = (f32[1024,128]{1,0:T(8,128)S(1)}, f32[1024,128]{1,0:T(8,128)S(1)}, u32[]{:S(2)}, u32[]{:S(2)}) collective-permute-start(f32[1024,128]{1,0:T(8,128)S(1)} %get-tuple-element.42), channel_id=1, source_target_pairs={{4,4},{12,20},{16,32},{20,36},{24,40},{28,44},{40,64},{48,76},{52,... | collective-permute-start | bytes 1572872 | tf_op jit(solution)/shard_map/ppermute | solution.py:403
  41.1 17.2 %collective-permute-start.17 = (f32[1536,128]{1,0:T(8,128)S(1)}, f32[1536,128]{1,0:T(8,128)S(1)}, u32[]{:S(2)}, u32[]{:S(2)}) collective-permute-start(f32[1536,128]{1,0:T(8,128)S(1)} %get-tuple-element.41), channel_id=1, source_target_pairs={{64,224},{68,228},{72,232},{76,236},{80,240},{84,244},{88,248},{92... | collective-permute-start | bytes 2359304 | tf_op jit(solution)/shard_map/ppermute | solution.py:403
  47.1 14.1 %collective-permute-start.11 = (f32[2048,128]{1,0:T(8,128)S(1)}, f32[2048,128]{1,0:T(8,128)S(1)}, u32[]{:S(2)}, u32[]{:S(2)}) collective-permute-start(f32[2048,128]{1,0:T(8,128)S(1)} %get-tuple-element.36), channel_id=1, source_target_pairs={{20,12},{40,32},{44,36},{48,40},{136,128},{148,140},{156,148},{172... | collective-permute-start | bytes 3145736 | tf_op jit(solution)/shard_map/ppermute | solution.py:403
  47.9 30.7 %collective-permute-start.14 = (f32[2048,128]{1,0:T(8,128)S(1)}, f32[2048,128]{1,0:T(8,128)S(1)}, u32[]{:S(2)}, u32[]{:S(2)}) collective-permute-start(f32[2048,128]{1,0:T(8,128)S(1)} %get-tuple-element.38), channel_id=1, source_target_pairs={{0,0},{4,12},{8,20},{12,24},{16,28},{20,32},{24,44},{28,48},{32,56... | collective-permute-start | bytes 3145736 | tf_op jit(solution)/shard_map/ppermute | solution.py:403
  56.4 42.9 %collective-permute-start.15 = (f32[2048,128]{1,0:T(8,128)S(1)}, f32[2048,128]{1,0:T(8,128)S(1)}, u32[]{:S(2)}, u32[]{:S(2)}) collective-permute-start(f32[2048,128]{1,0:T(8,128)S(1)} %get-tuple-element.39), channel_id=1, source_target_pairs={{0,0},{4,8},{8,16},{12,24},{16,32},{20,36},{28,48},{32,52},{36,60}... | collective-permute-start | bytes 3145736 | tf_op jit(solution)/shard_map/ppermute | solution.py:403
  58.3 1.4 collective-permute-start.7
  59.0 1.5 collective-permute-start.9
  59.7 40.9 %collective-permute-start.16 = (f32[2048,128]{1,0:T(8,128)S(1)}, f32[2048,128]{1,0:T(8,128)S(1)}, u32[]{:S(2)}, u32[]{:S(2)}) collective-permute-start(f32[2048,128]{1,0:T(8,128)S(1)} %get-tuple-element.40), channel_id=1, source_target_pairs={{0,4},{4,8},{8,16},{12,20},{16,28},{32,52},{36,56},{64,92},{72,100... | collective-permute-start | bytes 3145736 | tf_op jit(solution)/shard_map/ppermute | solution.py:403
  60.5 93.9 %collective-permute-start.4 = (f32[2048,128]{1,0:T(8,128)S(1)}, f32[2048,128]{1,0:T(8,128)S(1)}, u32[]{:S(2)}, u32[]{:S(2)}) collective-permute-start(f32[2048,128]{1,0:T(8,128)S(1)} %collective-permute-done.3), channel_id=1, source_target_pairs={{0,40},{4,48},{32,84},{36,88},{68,124},{176,188},{184,196},{160,20... | collective-permute-start | bytes 3145736 | tf_op jit(solution)/shard_map/ppermute | solution.py:403
  61.2 93.1 %collective-permute-start.12 = (f32[2048,128]{1,0:T(8,128)S(1)}, f32[2048,128]{1,0:T(8,128)S(1)}, u32[]{:S(2)}, u32[]{:S(2)}) collective-permute-start(f32[2048,128]{1,0:T(8,128)S(1)} %collective-permute-done.11), channel_id=1, source_target_pairs={{12,36},{32,64},{36,72},{40,76},{128,164},{140,172},{148,180},{164... | collective-permute-start | bytes 3145736 | tf_op jit(solution)/shard_map/ppermute | solution.py:403
  78.6 22.0 %collective-permute-start.1 = (f32[1536,128]{1,0:T(8,128)S(1)}, f32[1536,128]{1,0:T(8,128)S(1)}, u32[]{:S(2)}, u32[]{:S(2)}) collective-permute-start(f32[1536,128]{1,0:T(8,128)S(1)} %collective-permute-done), channel_id=1, source_target_pairs={{172,68},{176,76},{180,80},{224,128},{228,132},{232,136},{236,140}... | collective-permute-start | bytes 2359304 | tf_op jit(solution)/shard_map/ppermute | solution.py:403
  99.3 55.0 %collective-permute-start.18 = (f32[1536,128]{1,0:T(8,128)S(1)}, f32[1536,128]{1,0:T(8,128)S(1)}, u32[]{:S(2)}, u32[]{:S(2)}) collective-permute-start(f32[1536,128]{1,0:T(8,128)S(1)} %collective-permute-done.17), channel_id=1, source_target_pairs={{224,96},{228,100},{232,104},{236,108},{240,112},{244,116},{248,12... | collective-permute-start | bytes 2359304 | tf_op jit(solution)/shard_map/ppermute | solution.py:403
  160.8 5.9 %collective-permute-start.21 = (f32[40,128]{1,0:T(8,128)S(1)}, f32[40,128]{1,0:T(8,128)S(1)}, u32[]{:S(2)}, u32[]{:S(2)}) collective-permute-start(f32[40,128]{1,0:T(8,128)S(1)} %get-tuple-element.48), channel_id=1, source_target_pairs={{0,1},{1,2},{2,3},{3,0},{4,5},{5,6},{6,7},{7,4},{8,9},{9,10},{10,1... | collective-permute-start | bytes 61448 | tf_op jit(solution)/shard_map/ppermute | solution.py:407
  162.5 5.3 %collective-permute-start.22 = (f32[40,128]{1,0:T(8,128)S(1)}, f32[40,128]{1,0:T(8,128)S(1)}, u32[]{:S(2)}, u32[]{:S(2)}) collective-permute-start(f32[40,128]{1,0:T(8,128)S(1)} %get-tuple-element.49), channel_id=1, source_target_pairs={{0,2},{1,3},{2,0},{3,1},{4,6},{5,7},{6,4},{7,5},{8,10},{9,11},{10,... | collective-permute-start | bytes 61448 | tf_op jit(solution)/shard_map/ppermute | solution.py:407
  165.4 3.8 %collective-permute-start.23 = (f32[40,128]{1,0:T(8,128)S(1)}, f32[40,128]{1,0:T(8,128)S(1)}, u32[]{:S(2)}, u32[]{:S(2)}) collective-permute-start(f32[40,128]{1,0:T(8,128)S(1)} %get-tuple-element.50), channel_id=1, source_target_pairs={{0,3},{1,0},{2,1},{3,2},{4,7},{5,4},{6,5},{7,6},{8,11},{9,8},{10,9... | collective-permute-start | bytes 61448 | tf_op jit(solution)/shard_map/ppermute | solution.py:407
  (1 other events, 2.2 us)
